TPU v7x, 256 devices: a whole 4x4x8 slice. The times are simulated.
256 devices in a mesh: occ: 16 (over z_lo, x), vir: 16 (over z_hi, y, core).
Axes of the slice: x: 4, y: 4, z: 8 (z_hi: 2, z_lo: 4; z = z_hi * 4 + z_lo), core: 2. Of those that a mesh axis runs over, the one named last changes fastest.
Arguments:
- b_occ: bfloat16 [64, 768, 2304], P('occ', 'vir'), may hold values from -0.86328125 to 0.86328125
- b_outer: bfloat16 [2, 768, 2304], P(None, 'vir', 'occ'), may hold values from -0.86328125 to 0.86328125
- eps_occ: float32 [64], P('occ'), may hold values from -1.5 to -0.3
- eps_outer: float32 [2], replicated, may hold values from -1.5 to -0.3
- eps_vir: float32 [768], P('vir'), may hold values from 0.2 to 3
Outputs:
- gamma_occ: float32 [64, 768, 2304], P('occ', 'vir')
- gamma_outer: float32 [2, 768, 2304], P(None, 'vir', 'occ')
All inputs are finite; a program needn't handle non-finite values.
Results may differ from a plain program's by a relative error of at most 0.0018.
Values may be sent and summed in bfloat16 or wider, within the bound.
No kernel may reach another device: no remote copies, remote signals or barrier semaphores. Data moves between devices by JAX's collectives and lax.ppermute only.
A program may use at most 128 MiB of HBM per device.

v0:
```python
import jax
import jax.numpy as jnp
from jax import lax
from jax.sharding import PartitionSpec as P


def in_order(tiles, dim):
    shape = list(tiles.shape[1:])
    shape[dim] *= tiles.shape[0]
    return jnp.moveaxis(tiles, 0, dim).reshape(shape)


def from_everyone(array, axis):
    devices = lax.axis_size(axis)
    return lax.all_to_all(
        jnp.broadcast_to(array[None], (devices, *array.shape)), axis, 0, 0, tiled=True
    )


def collect(array, axis, dim):
    return in_order(from_everyone(array, axis), dim)


def cut_along(array, dim, devices):
    shape = array.shape
    tiles = array.reshape(*shape[:dim], devices, shape[dim] // devices, *shape[dim + 1 :])
    return jnp.moveaxis(tiles, dim, 0)


def sum_at_owner(array, axis, dim):
    tiles = cut_along(array, dim, lax.axis_size(axis))
    arrived = lax.all_to_all(tiles, axis, split_axis=0, concat_axis=0, tiled=True)
    return arrived.sum(axis=0)


def on_device(b_occ, b_outer, eps_occ, eps_outer, eps_vir):
    aux_full = collect(b_outer, "occ", 2)
    b_whole, eps_whole = (
        lax.all_gather(aux_full, "vir", axis=1, tiled=True),
        lax.all_gather(eps_vir.astype(jnp.bfloat16), "vir", axis=0, tiled=True).astype(
            eps_vir.dtype
        ),
    )
    integral = jnp.einsum("iaq,jbq->ijab", b_occ, b_whole, preferred_element_type=jnp.float32)
    denom = (
        eps_occ[:, None, None, None]
        + eps_outer[None, :, None, None]
        - eps_vir[None, None, :, None]
        - eps_whole[None, None, None, :]
    )
    amps = integral / denom
    received = lax.all_to_all(amps, "vir", split_axis=3, concat_axis=2, tiled=True)
    swapped = jnp.swapaxes(received, 2, 3)
    tilde = 2.0 * amps - swapped
    whole_wide = b_whole.astype(jnp.float32)
    occ_wide = b_occ.astype(jnp.float32)
    gamma_occ = jnp.einsum("ijab,jbq->iaq", tilde, whole_wide, precision=lax.Precision.HIGHEST)
    partial_terms = jnp.einsum("ijab,iaq->jbq", tilde, occ_wide, precision=lax.Precision.HIGHEST)
    section = lax.psum_scatter(partial_terms, "occ", scatter_dimension=2, tiled=True)
    gamma_outer = sum_at_owner(section, "vir", 1)
    return (gamma_occ, gamma_outer)


def solution(mesh):
    placed = (P("occ", "vir", None), P(None, "vir", "occ"), P("occ"), P(), P("vir"))
    return jax.shard_map(
        on_device,
        mesh=mesh,
        in_specs=placed,
        out_specs=(P("occ", "vir", None), P(None, "vir", "occ")),
        check_vma=False,
    )
```

profile of v0, /device:TPU:57, one launch (start us, length us, event | category | flops | bytes accessed | tf_op | source)
XLA Modules:
  0.0 437.4 jit_solution(1682618729027701697)
XLA Ops:
  7.2 0.0 copy-start
  7.2 0.0 all-gather.2.cloned.1.call-start
  7.2 0.9 broadcast_in_dim.2
  8.2 27.7 %all_to_all.28 = bf16[16,2,48,144]{3,2,1,0:T(8,128)(2,1)S(1)} all-to-all(bf16[16,2,48,144]{3,2,1,0:T(8,128)(2,1)S(1)} %broadcast_in_dim.2), channel_id=1, replica_groups=mesh['occ'=16,'vir'=16] {'occ'}, dimensions={0} | all-to-all | bytes 884736 | tf_op jit(solution)/shard_map/all_to_all | solution.py:15
  35.8 0.4 copy.12
  36.3 0.0 copy-start.3
  36.3 0.0 copy-start.4
  36.3 0.0 copy-start.1
  36.3 0.0 copy-start.2
  36.3 1.9 reshape.51
  38.2 0.0 all-gather.2.cloned.1.call-update
  38.2 0.0 reduce-scatter.2.cloned.1.call-start
  38.3 0.0 copy-done.3
  38.3 0.0 copy-done.4
  38.3 0.6 dynamic-slice
  39.6 0.2 dynamic-update-slice
  39.8 44.7 %all-reduce = bf16[768]{0:T(1024)(128)(2,1)S(1)} all-reduce(bf16[768]{0:T(1024)(128)(2,1)S(1)} %dynamic-update-slice), channel_id=1, replica_groups=mesh['occ'=16,'vir'=16] {'vir'}, use_global_device_ids=true, to_apply=%add | all-reduce | flops 768 | bytes 3072
  84.5 0.0 copy-done.1
  84.5 0.0 copy-done.2
  84.5 0.1 broadcast_add_fusion
  84.5 0.1 broadcast_subtract_fusion
  84.6 51.1 %all-gather.2.cloned.1.call-done = bf16[2,768,2304]{2,1,0:T(8,128)(2,1)} async-done(((bf16[2,48,2304]{2,1,0:T(8,128)(2,1)}), bf16[2,768,2304]{2,1,0:T(8,128)(2,1)}) %all-gather.2.cloned.1.call-update) | async-done | bytes 7077904 | tf_op jit(solution)/shard_map/all_gather | solution.py:39
  135.7 0.0 copy-done
  135.7 5.4 %fusion.10 = f32[4,2,48,768]{3,2,0,1:T(8,128)S(1)} fusion(bf16[2,768,2304]{2,1,0:T(8,128)(2,1)} %all-gather.2.cloned.1.call-done, bf16[4,48,2304]{2,1,0:T(8,128)(2,1)S(1)} %copy-done, f32[768]{0:T(1024)S(1)} %convert_element_type.9, f32[4,2,48]{2,0,1:T(4,128)S(1)} %broadcast_subtract_fusion), kind=kOutput, calls=%fused_computation.8 | convolution fusion | flops 1359544320 | bytes 9146880 | tf_op jit(solution)/shard_map/iaq,jbq->ijab/dot_general | solution.py:44
  141.1 2.7 copy.13
  143.9 5.7 %reshape.62 = f32[16,1,18432]{2,1,0:T(1,128)} reshape(f32[768,2,4,48]{3,2,1,0:T(4,128)} %bitcast.50) | data formatting | bytes 2359296
  149.6 35.7 %all_to_all.29 = f32[16,1,18432]{2,1,0:T(1,128)S(1)} all-to-all(f32[16,1,18432]{2,1,0:T(1,128)} %reshape.62), channel_id=1, replica_groups=mesh['occ'=16,'vir'=16] {'vir'}, dimensions={0} | all-to-all | bytes 2359296 | tf_op jit(solution)/shard_map/all_to_all | solution.py:52
  185.3 0.5 broadcast.39
  185.9 4.8 %reduce = f32[16,18432]{1,0:T(8,128)} reduce(f32[16,1,18432]{2,1,0:T(1,128)S(1)} %all_to_all.29, f32[]{:T(128)} %broadcast.39), dimensions={1}, to_apply=%all_to_all.20.reduce_sub_computation | reduce | bytes 2359300 | tf_op jit(solution)/shard_map/all_to_all | solution.py:52
  190.6 5.4 %reshape.63 = f32[768,2,4,48]{3,2,1,0:T(4,128)} reshape(f32[16,18432]{1,0:T(8,128)} %reduce) | data formatting | bytes 2359296
  196.0 5.4 %copy.20 = f32[4,2,48,16,48]{2,3,4,0,1:T(8,128)} copy(f32[4,2,48,16,48]{2,0,1,4,3:T(4,128)} %bitcast.48) | data formatting | bytes 2359296 | tf_op jit(solution)/shard_map/all_to_all | solution.py:52
  201.4 2.8 all_to_all.23
  204.2 9.0 %convolution_bitcast_fusion = f32[2,768,2304]{1,2,0:T(8,128)} fusion(bf16[4,48,2304]{2,1,0:T(8,128)(2,1)S(1)} %copy-done, f32[4,2,768,48]{2,3,0,1:T(8,128)S(1)} %all_to_all.23, f32[4,2,48,768]{3,2,0,1:T(8,128)S(1)} %fusion.10), kind=kOutput, calls=%fused_computation | convolution fusion | flops 8154316800 | bytes 17399808 | tf_op jit(solution)/shard_map/ijab,iaq->jbq/dot_general | solution.py:58
  213.3 0.0 reduce-scatter.2.cloned.1.call-update
  213.3 156.7 %reduce-scatter.2.cloned.1.call-done = f32[2,768,144]{1,2,0:T(8,128)} async-done(((f32[2,768,2304]{1,2,0:T(8,128)}), f32[2,768,144]{1,2,0:T(8,128)}) %reduce-scatter.2.cloned.1.call-update) | async-done | bytes 884752 | tf_op jit(solution)/shard_map/reduce_scatter | solution.py:59
  370.0 2.8 copy.15
  372.8 2.7 copy.16
  375.5 10.3 %all-to-all-start.2 = ((f32[16,2,48,144]{3,2,1,0:T(8,128)}), f32[16,2,48,144]{3,2,1,0:T(8,128)}, u32[]{:S(2)}, u32[]{:S(2)}) async-start(f32[16,2,48,144]{3,2,1,0:T(8,128)} %copy.16), calls=%async_computation.3 | async-start | bytes 3145728 | tf_op jit(solution)/shard_map/all_to_all | solution.py:32
  385.8 7.7 %fusion.4 = f32[4,48,2304]{2,1,0:T(8,128)} fusion(bf16[2,768,2304]{2,1,0:T(8,128)(2,1)} %all-gather.2.cloned.1.call-done, f32[4,2,768,48]{2,3,0,1:T(8,128)S(1)} %all_to_all.23, f32[4,2,48,768]{3,2,0,1:T(8,128)S(1)} %fusion.10), kind=kOutput, calls=%fused_computation.5 | convolution fusion | flops 8154316800 | bytes 11206656 | tf_op jit(solution)/shard_map/ijab,jbq->iaq/dot_general | solution.py:57
  393.5 34.9 %all-to-all-done.2 = f32[16,2,48,144]{3,2,1,0:T(8,128)} async-done(((f32[16,2,48,144]{3,2,1,0:T(8,128)}), f32[16,2,48,144]{3,2,1,0:T(8,128)}, u32[]{:S(2)}, u32[]{:S(2)}) %all-to-all-start.2) | async-done | bytes 884768 | tf_op jit(solution)/shard_map/all_to_all | solution.py:32
  428.4 2.2 reduce_sum.9
  (3 shorter events, 0.0 us)
Async XLA Ops:
  7.2 128.5 %copy-start = (bf16[4,48,2304]{2,1,0:T(8,128)(2,1)S(1)}, bf16[4,48,2304]{2,1,0:T(8,128)(2,1)}, u32[]{:S(2)}) copy-start(bf16[4,48,2304]{2,1,0:T(8,128)(2,1)} %param.5) | copy-start | bytes 2654212
  7.2 128.5 %all-gather.2.cloned.1.call-start = ((), (), s32[]{:S(2)}) async-start(), calls=%async_computation.4 | async-start | bytes 7520256 | tf_op jit(solution)/shard_map/all_gather | solution.py:39
  36.3 2.0 copy-start.3
  36.3 2.0 copy-start.4
  36.3 48.2 %copy-start.1 = (f32[4]{0:T(128)S(1)}, f32[4]{0:T(128)}, u32[]{:S(2)}) copy-start(f32[4]{0:T(128)} %param.7) | copy-start | bytes 52
  36.3 48.2 %copy-start.2 = (f32[2]{0:T(128)S(1)}, f32[2]{0:T(128)}, u32[]{:S(2)}) copy-start(f32[2]{0:T(128)} %param.8) | copy-start | bytes 28
  38.2 331.8 %reduce-scatter.2.cloned.1.call-start = ((), (), s32[]{:S(2)}) async-start(), calls=%async_computation.5 | async-start | bytes 15040512 | tf_op jit(solution)/shard_map/reduce_scatter | solution.py:59
  375.5 53.0 %all-to-all-start.2 = ((f32[16,2,48,144]{3,2,1,0:T(8,128)}), f32[16,2,48,144]{3,2,1,0:T(8,128)}, u32[]{:S(2)}, u32[]{:S(2)}) async-start(f32[16,2,48,144]{3,2,1,0:T(8,128)} %copy.16), calls=%async_computation.3 | async-start | bytes 3145728 | tf_op jit(solution)/shard_map/all_to_all | solution.py:32
Sparse Core Ops, SparseCore 0:
  38.3 97.3 all-gather.1
  213.4 156.5 reduce-scatter.1
where the time goes:
time: 438 us; the launch traced here: 437 us
  waiting for transfers between devices  243 us (55%)
  blocking collectives  108 us (25%)
  local copies, waits for them, and re-layouts  32.1 us (7%)
  matrix products  22.2 us (5%)
  between operations  14.8 us (3%)
  starting transfers between devices  10.4 us (2%)
  other arithmetic  7.1 us (2%)
    reduce_scatter x1, waiting for transfers between devices, on_device(): lax.psum_scatter(partial_terms, 'occ', scatter_dimension=2, tiled=True)  157 us
    all_gather x1, waiting for transfers between devices, on_device(): lax.all_gather(aux_full, 'vir', axis=1, tiled=True)  51.1 us
    unnamed x1, blocking collectives  44.7 us
    all_to_all x1, blocking collectives, on_device(): lax.all_to_all(amps, 'vir', split_axis=3, concat_axis=2, tiled=True)  35.7 us
    all_to_all x1, waiting for transfers between devices, sum_at_owner(): lax.all_to_all(tiles, axis, split_axis=0, concat_axis=0, tiled=True)  34.9 us
    all_to_all x1, blocking collectives, from_everyone(): lax.all_to_all(jnp.broadcast_to(array[None], (devices, *array.shape)), ax...  27.7 us
    unnamed x15, local copies, waits for them, and re-layouts  12 us
    all_to_all x1, starting transfers between devices, sum_at_owner(): lax.all_to_all(tiles, axis, split_axis=0, concat_axis=0, tiled=True)  10.3 us
  transfers between devices with their start and end apart: 3, of which 3 were waited for; matrix products, arithmetic and copies ran while one was open for 2% of the time, Pallas kernels for 0%

commit v1 on v0

--- a/solution.py
+++ b/solution.py
@@ -36,7 +36,9 @@
 def on_device(b_occ, b_outer, eps_occ, eps_outer, eps_vir):
     aux_full = collect(b_outer, "occ", 2)
     b_whole, eps_whole = (
-        lax.all_gather(aux_full, "vir", axis=1, tiled=True),
+        jnp.concatenate(
+            lax.all_to_all(jnp.stack([aux_full] * lax.axis_size("vir")), "vir", 0, 0), axis=1
+        ),
         lax.all_gather(eps_vir.astype(jnp.bfloat16), "vir", axis=0, tiled=True).astype(
             eps_vir.dtype
         ),

time: 438 us -> 556 us (1.27)
  blocking collectives: 108 us -> 264 us
  waiting for transfers between devices: 243 us -> 188 us
  starting transfers between devices: 10.4 us -> 20.6 us
  local copies, waits for them, and re-layouts: 32.1 us -> 41.3 us
    unnamed x1, blocking collectives: 44.7 us -> 204 us
    all_gather x1 -> x0, waiting for transfers between devices: 51.1 us -> none  [on_device(): lax.all_gather(aux_full, 'vir', axis=1, tiled=True)]
    all_to_all x0 -> x1, starting transfers between devices: none -> 10.3 us  [on_device(): lax.all_to_all(jnp.stack([aux_full] * lax.axis_size('vir')), 'vir', 0, 0)]
    unnamed x15 -> x17, local copies, waits for them, and re-layouts: 12 us -> 14.8 us
  transfers between devices with their start and end apart: 3 -> 3, of which waited for: 3 -> 2; matrix products, arithmetic and copies ran while one was open for 2% -> 2% of each run, Pallas kernels for 0% -> 0%
where the time goes in v1:
time: 556 us; the launch traced here: 555 us
  blocking collectives  264 us (47%)
  waiting for transfers between devices  188 us (34%)
  local copies, waits for them, and re-layouts  41.3 us (7%)
  starting transfers between devices  20.6 us (4%)
  matrix products  19.2 us (3%)
  between operations  14.8 us (3%)
  other arithmetic  7.1 us (1%)
    unnamed x1, blocking collectives  204 us
    reduce_scatter x1, waiting for transfers between devices, on_device(): lax.psum_scatter(partial_terms, 'occ', scatter_dimension=2, tiled=True)  153 us
    all_to_all x1, waiting for transfers between devices, sum_at_owner(): lax.all_to_all(tiles, axis, split_axis=0, concat_axis=0, tiled=True)  35.1 us
    all_to_all x1, blocking collectives, on_device(): lax.all_to_all(amps, 'vir', split_axis=3, concat_axis=2, tiled=True)  33 us
    all_to_all x1, blocking collectives, from_everyone(): lax.all_to_all(jnp.broadcast_to(array[None], (devices, *array.shape)), ax...  27.7 us
    unnamed x17, local copies, waits for them, and re-layouts  14.8 us
  transfers between devices with their start and end apart: 3, of which 2 were waited for; matrix products, arithmetic and copies ran while one was open for 2% of the time, Pallas kernels for 0%

profile of v1, /device:TPU:57, one launch (start us, length us, event | category | flops | bytes accessed | tf_op | source)
XLA Modules:
  0.0 555.4 jit_solution(16944449736523267549)
XLA Ops:
  7.2 0.0 copy-start
  7.2 0.9 broadcast_in_dim.2
  8.1 27.7 %all_to_all.33 = bf16[16,2,48,144]{3,2,1,0:T(8,128)(2,1)S(1)} all-to-all(bf16[16,2,48,144]{3,2,1,0:T(8,128)(2,1)S(1)} %broadcast_in_dim.2), channel_id=1, replica_groups=mesh['occ'=16,'vir'=16] {'occ'}, dimensions={0} | all-to-all | bytes 884736 | tf_op jit(solution)/shard_map/all_to_all | solution.py:15
  35.8 0.4 copy.17
  36.2 1.1 stack_reshape.2
  37.3 3.6 stack.3
  41.0 0.0 copy-start.4
  41.0 0.0 copy-start.5
  41.0 0.0 copy-start.2
  41.0 0.0 copy-start.3
  41.0 10.3 %all-to-all-start.1 = ((bf16[16,2,48,2304]{3,2,1,0:T(8,128)(2,1)}), bf16[16,2,48,2304]{3,2,1,0:T(8,128)(2,1)}, u32[]{:S(2)}, u32[]{:S(2)}) async-start(bf16[16,2,48,2304]{3,2,1,0:T(8,128)(2,1)} %stack.3), calls=%async_computation.1 | async-start | bytes 14155776 | tf_op jit(solution)/shard_map/all_to_all | solution.py:40
  51.2 0.0 reduce-scatter.2.cloned.1.call-start
  51.3 0.0 copy-done.4
  51.3 0.0 copy-done.5
  51.3 0.6 dynamic-slice
  52.6 0.2 dynamic-update-slice
  52.8 203.8 %all-reduce = bf16[768]{0:T(1024)(128)(2,1)S(1)} all-reduce(bf16[768]{0:T(1024)(128)(2,1)S(1)} %dynamic-update-slice), channel_id=1, replica_groups=mesh['occ'=16,'vir'=16] {'vir'}, use_global_device_ids=true, to_apply=%add | all-reduce | flops 768 | bytes 3072
  256.6 0.0 copy-done.2
  256.6 0.0 copy-done.3
  256.6 0.1 broadcast_add_fusion
  256.7 0.1 broadcast_subtract_fusion
  256.8 0.0 all-to-all-done.1
  256.8 3.5 copy.18
  260.3 0.0 copy-start.1
  260.3 2.8 copy-done.1
  263.1 0.0 copy-done
  263.1 2.4 fusion
  265.5 2.7 copy.19
  268.3 5.7 %reshape.68 = f32[16,1,18432]{2,1,0:T(1,128)} reshape(f32[768,2,4,48]{3,2,1,0:T(4,128)} %bitcast.47) | data formatting | bytes 2359296
  274.0 33.0 %all_to_all.34 = f32[16,1,18432]{2,1,0:T(1,128)S(1)} all-to-all(f32[16,1,18432]{2,1,0:T(1,128)} %reshape.68), channel_id=1, replica_groups=mesh['occ'=16,'vir'=16] {'vir'}, dimensions={0} | all-to-all | bytes 2359296 | tf_op jit(solution)/shard_map/all_to_all | solution.py:54
  307.0 0.5 broadcast.40
  307.5 4.8 reduce
  312.3 5.4 reshape.69
  317.7 5.4 copy.26
  323.1 2.8 all_to_all.27
  325.9 9.0 %convolution_bitcast_fusion = f32[2,768,2304]{1,2,0:T(8,128)} fusion(bf16[4,48,2304]{2,1,0:T(8,128)(2,1)S(1)} %copy-done, f32[4,2,768,48]{2,3,0,1:T(8,128)S(1)} %all_to_all.27, f32[4,2,48,768]{3,2,0,1:T(8,128)S(1)} %fusion), kind=kOutput, calls=%fused_computation | convolution fusion | flops 8154316800 | bytes 17399808 | tf_op jit(solution)/shard_map/ijab,iaq->jbq/dot_general | solution.py:60
  334.9 0.0 reduce-scatter.2.cloned.1.call-update
  334.9 152.8 %reduce-scatter.2.cloned.1.call-done = f32[2,768,144]{1,2,0:T(8,128)} async-done(((f32[2,768,2304]{1,2,0:T(8,128)}), f32[2,768,144]{1,2,0:T(8,128)}) %reduce-scatter.2.cloned.1.call-update) | async-done | bytes 884752 | tf_op jit(solution)/shard_map/reduce_scatter | solution.py:61
  487.8 2.8 copy.21
  490.6 2.7 copy.22
  493.3 10.3 %all-to-all-start.3 = ((f32[16,2,48,144]{3,2,1,0:T(8,128)}), f32[16,2,48,144]{3,2,1,0:T(8,128)}, u32[]{:S(2)}, u32[]{:S(2)}) async-start(f32[16,2,48,144]{3,2,1,0:T(8,128)} %copy.22), calls=%async_computation.4 | async-start | bytes 3145728 | tf_op jit(solution)/shard_map/all_to_all | solution.py:32
  503.6 7.7 %convolution_bitcast_fusion.1 = f32[4,48,2304]{2,1,0:T(8,128)} fusion(bf16[2,768,2304,1]{2,1,3,0:T(8,128)(2,1)} %bitcast.44, f32[4,2,768,48]{2,3,0,1:T(8,128)S(1)} %all_to_all.27, f32[4,2,48,768]{3,2,0,1:T(8,128)S(1)} %fusion), kind=kOutput, calls=%fused_computation.1 | convolution fusion | flops 8154316800 | bytes 11206656 | tf_op jit(solution)/shard_map/ijab,jbq->iaq/dot_general | solution.py:59
  511.3 35.1 %all-to-all-done.3 = f32[16,2,48,144]{3,2,1,0:T(8,128)} async-done(((f32[16,2,48,144]{3,2,1,0:T(8,128)}), f32[16,2,48,144]{3,2,1,0:T(8,128)}, u32[]{:S(2)}, u32[]{:S(2)}) %all-to-all-start.3) | async-done | bytes 884768 | tf_op jit(solution)/shard_map/all_to_all | solution.py:32
  546.4 2.2 reduce_sum.9
  (3 shorter events, 0.0 us)
Async XLA Ops:
  7.2 255.9 %copy-start = (bf16[4,48,2304]{2,1,0:T(8,128)(2,1)S(1)}, bf16[4,48,2304]{2,1,0:T(8,128)(2,1)}, u32[]{:S(2)}) copy-start(bf16[4,48,2304]{2,1,0:T(8,128)(2,1)} %param.5) | copy-start | bytes 2654212
  41.0 10.3 %copy-start.4 = (f32[48]{0:T(128)S(1)}, f32[48]{0:T(128)}, u32[]{:S(2)}) copy-start(f32[48]{0:T(128)} %param.9) | copy-start | bytes 580
  41.0 10.3 %copy-start.5 = (u32[256]{0:T(256)S(1)}, u32[256]{0:T(256)}, u32[]{:S(2)}) copy-start(u32[256]{0:T(256)} %constant.8) | copy-start | bytes 3076
  41.0 215.7 %copy-start.2 = (f32[4]{0:T(128)S(1)}, f32[4]{0:T(128)}, u32[]{:S(2)}) copy-start(f32[4]{0:T(128)} %param.7) | copy-start | bytes 52
  41.0 215.7 %copy-start.3 = (f32[2]{0:T(128)S(1)}, f32[2]{0:T(128)}, u32[]{:S(2)}) copy-start(f32[2]{0:T(128)} %param.8) | copy-start | bytes 28
  41.0 215.8 %all-to-all-start.1 = ((bf16[16,2,48,2304]{3,2,1,0:T(8,128)(2,1)}), bf16[16,2,48,2304]{3,2,1,0:T(8,128)(2,1)}, u32[]{:S(2)}, u32[]{:S(2)}) async-start(bf16[16,2,48,2304]{3,2,1,0:T(8,128)(2,1)} %stack.3), calls=%async_computation.1 | async-start | bytes 14155776 | tf_op jit(solution)/shard_map/all_to_all | solution.py:40
  51.2 436.6 %reduce-scatter.2.cloned.1.call-start = ((), (), s32[]{:S(2)}) async-start(), calls=%async_computation.5 | async-start | bytes 15040512 | tf_op jit(solution)/shard_map/reduce_scatter | solution.py:61
  260.3 2.8 copy-start.1
  493.3 53.1 %all-to-all-start.3 = ((f32[16,2,48,144]{3,2,1,0:T(8,128)}), f32[16,2,48,144]{3,2,1,0:T(8,128)}, u32[]{:S(2)}, u32[]{:S(2)}) async-start(f32[16,2,48,144]{3,2,1,0:T(8,128)} %copy.22), calls=%async_computation.4 | async-start | bytes 3145728 | tf_op jit(solution)/shard_map/all_to_all | solution.py:32
Sparse Core Ops, SparseCore 0:
  335.1 152.6 reduce-scatter.1
